TPU v7x, 32 devices: a whole 2x2x4 slice. The times are simulated.
32 devices in a mesh: gx: 2 (over x), gy: 4 (over y, core), gz: 4 (over z).
Axes of the slice: x: 2, y: 2, z: 4, core: 2. Of those that a mesh axis runs over, the one named last changes fastest.
Arguments:
- features: bfloat16 [256, 4096], P('gz', ('gy', 'gx')), may hold values from -14 to 14, as said below
- tiles: bfloat16 [32, 32, 128, 128], P('gx', 'gy'), may hold values from -0.5 to 0.5
- block_mask: int32 [32, 32], P('gx', 'gy'), may hold values from 0 to 1, as said below
- tile_counts: int32 [32], P('gx'), may hold values from 1 to 32, as said below
- weight: bfloat16 [256, 256], replicated, may hold values from -0.375 to 0.375
- gamma: float32 [256], P('gz'), may hold values from 0.5 to 2
- beta: float32 [256], P('gz'), may hold values from -3 to 3
Outputs:
- normed: bfloat16 [256, 4096], P('gz', ('gx', 'gy'))
Inputs may be any that keep to these rules, and one draw needn't show every extreme that they name: `features`: channels along dimension 0, nodes along dimension 1. `block_mask`: 1 where block row and block column meet in a nonzero block, else 0; the diagonal is 1. tile_counts[r] is the number of ones in row r of block_mask.
All inputs are finite; a program needn't handle non-finite values.
Results may differ from a plain program's by a relative error of at most 0.013.
Values may be sent and summed in bfloat16 or wider, within the bound.
A program may use at most 64 MiB of HBM per device.

v0:
```python
import jax
import jax.numpy as jnp
from jax import lax
from jax.sharding import PartitionSpec as P


def body(features, tiles, block_mask, tile_counts, weight, gamma, beta):
    panel = lax.all_gather(features, "gx", axis=1, tiled=True)
    local_ch = panel.shape[0]
    rows_blk = tiles.shape[0]
    cols_blk = tiles.shape[1]
    tile_len = tiles.shape[2]
    panels = panel.reshape(local_ch, cols_blk, tile_len)
    prods = jnp.einsum("fcn,rcmn->frcm", panels, tiles, preferred_element_type=jnp.float32)
    share = block_mask.astype(jnp.float32) / tile_counts.astype(jnp.float32)[:, None]
    partial_value = jnp.einsum("frcm,rc->frm", prods, share).reshape(local_ch, rows_blk * tile_len)
    summed = lax.psum(partial_value, "gy")
    width = rows_blk * tile_len // lax.axis_size("gy")
    agg = lax.dynamic_slice_in_dim(summed, lax.axis_index("gy") * width, width, 1)
    agg = agg.astype(jnp.bfloat16)
    offset = lax.axis_index("gz") * local_ch
    full = lax.all_gather(agg, "gz", axis=0, tiled=True)
    w_cols = lax.dynamic_slice_in_dim(weight, offset, local_ch, 1)
    z_vals = jnp.einsum("co,cn->on", w_cols, full, preferred_element_type=jnp.float32)
    total = z_vals.shape[1] * lax.axis_size(("gx", "gy"))
    sums, squares = lax.psum(
        (jnp.sum(z_vals, axis=1), jnp.sum(z_vals * z_vals, axis=1)), ("gx", "gy")
    )
    mean = sums / total
    var = squares / total - mean * mean
    centered = z_vals - mean[:, None]
    scaled = gamma[:, None] * centered * lax.rsqrt(var + 1e-05)[:, None] + beta[:, None]
    return jnp.maximum(scaled, 0.0).astype(jnp.bfloat16)


def solution(mesh):
    in_specs = (
        P("gz", ("gy", "gx")),
        P("gx", "gy", None, None),
        P("gx", "gy"),
        P("gx"),
        P(),
        P("gz"),
        P("gz"),
    )
    out_specs = P("gz", ("gx", "gy"))
    return jax.shard_map(body, mesh=mesh, in_specs=in_specs, out_specs=out_specs, check_vma=False)
```

profile of v0, /device:TPU:0, one launch (start us, length us, event | category | flops | bytes accessed | tf_op | source)
XLA Modules:
  0.0 57.3 jit_solution(9171550169248883873)
XLA Ops:
  0.0 0.0 copy-start
  0.0 0.7 %convert_element_type.13 = f32[16]{0:T(128)S(1)} convert(s32[16]{0:T(128)} %param.10) | non-fusion elementwise | flops 16 | bytes 128 | tf_op jit(solution)/shard_map/convert_element_type | solution.py:15
  0.7 0.7 %divide_bitcast_fusion = bf16[16,8,1,1]{0,1,2,3:T(8,128)(2,1)S(1)} fusion(s32[16,8]{0,1:T(8,128)} %param.9, f32[16]{0:T(128)S(1)} %convert_element_type.13), kind=kLoop, calls=%fused_computation.12 | loop fusion | flops 384 | bytes 832 | tf_op jit(solution)/shard_map/div | solution.py:15
  1.4 0.1 copy.12
  1.5 6.1 %all_gather.6 = bf16[64,1024]{1,0:T(8,128)(2,1)S(1)} all-gather(bf16[64,512]{1,0:T(8,128)(2,1)} %param.7), channel_id=1, replica_groups=mesh['gx'=2,'gy'=4,'gz'=4] {'gx'}, dimensions={1}, use_global_device_ids=true | all-gather | bytes 196608 | tf_op jit(solution)/shard_map/all_gather | solution.py:8
  7.6 3.8 %fusion.4 = bf16[64,16,8,128]{3,0,1,2:T(8,128)(2,1)S(1)} fusion(bf16[16,8,128,128]{3,2,1,0:T(8,128)(2,1)} %param.8, bf16[64,8,128,1]{2,1,0,3:T(8,128)(2,1)S(1)} %bitcast.19), kind=kOutput, calls=%fused_computation.4 | convolution fusion | flops 268435456 | bytes 6422528 | tf_op jit(solution)/shard_map/fcn,rcmn->frcm/dot_general | solution.py:14
  11.4 1.4 %fusion = f32[16,1,64,128]{3,1,2,0:T(1,128)S(1)} fusion(bf16[16,8,1,1]{1,2,3,0:T(2,128)(2,1)S(1)} %copy.12, bf16[64,16,8,128]{3,0,1,2:T(8,128)(2,1)S(1)} %fusion.4), kind=kOutput, calls=%fused_computation | convolution fusion | flops 2097152 | bytes 2621696 | tf_op jit(solution)/shard_map/frcm,rc->frm/dot_general | solution.py:16
  12.8 0.0 copy-start.1
  12.8 0.0 copy-start.2
  12.8 0.3 copy.14
  13.2 0.2 copy.28
  13.3 16.7 %all-reduce.2 = bf16[64,2048]{1,0:T(8,128)(2,1)S(1)} all-reduce(f32[64,2048]{1,0:T(8,128)S(1)} %bitcast.18), channel_id=1, replica_groups=mesh['gx'=2,'gy'=4,'gz'=4] {'gy'}, use_global_device_ids=true, to_apply=%region_0.0 | all-reduce | flops 131072 | bytes 786432 | tf_op jit(solution)/shard_map/psum | solution.py:17
  30.1 14.2 %all_gather.7 = bf16[256,512]{1,0:T(8,128)(2,1)S(1)} all-gather(bf16[64,512]{1,0:T(8,128)(2,1)S(1)} %dynamic-slice_convert_fusion), channel_id=1, replica_groups=mesh['gx'=2,'gy'=4,'gz'=4] {'gz'}, dimensions={0}, use_global_device_ids=true | all-gather | bytes 327680 | tf_op jit(solution)/shard_map/all_gather | solution.py:22
  44.3 0.0 copy-done
  44.3 0.4 fusion.11
  44.7 11.8 %all-reduce = (f32[64]{0:T(128)S(1)}, f32[64]{0:T(128)S(1)}) all-reduce(f32[64]{0:T(128)S(1)} %get-tuple-element.6, f32[64]{0:T(128)S(1)} %get-tuple-element.5), channel_id=1, replica_groups=mesh['gx'=2,'gy'=4,'gz'=4] {'gx','gy'}, use_global_device_ids=true, to_apply=%region_4.0 | all-reduce | flops 128 | bytes 1024 | tf_op jit(solution)/shard_map/psum | solution.py:26
  56.5 0.0 copy-done.1
  56.5 0.0 copy-done.2
  56.5 0.7 %maximum_convert_fusion = bf16[64,512]{1,0:T(8,128)(2,1)} fusion(f32[64,512]{1,0:T(8,128)S(1)} %get-tuple-element.11, f32[64]{0:T(128)S(1)} %copy-done.1, f32[64]{0:T(128)S(1)} %get-tuple-element.10, f32[64]{0:T(128)S(1)} %get-tuple-element.9, f32[64]{0:T(128)S(1)} %copy-done.2), kind=kLoop, calls=%fused_computation.7 | loop fusion | flops 196608 | bytes 197632 | tf_op jit(solution)/shard_map/convert_element_type | solution.py:33
  (3 shorter events, 0.0 us)
Async XLA Ops:
  0.0 44.3 %copy-start = (bf16[256,256]{1,0:T(8,128)(2,1)S(1)}, bf16[256,256]{1,0:T(8,128)(2,1)}, u32[]{:S(2)}) copy-start(bf16[256,256]{1,0:T(8,128)(2,1)} %param.11) | copy-start | bytes 393220
  12.8 43.7 %copy-start.1 = (f32[64]{0:T(128)S(1)}, f32[64]{0:T(128)}, u32[]{:S(2)}) copy-start(f32[64]{0:T(128)} %param.13) | copy-start | bytes 772
  12.8 43.7 %copy-start.2 = (f32[64]{0:T(128)S(1)}, f32[64]{0:T(128)}, u32[]{:S(2)}) copy-start(f32[64]{0:T(128)} %param.12) | copy-start | bytes 772
where the time goes:
time: 57.5 us; the launch traced here: 57.3 us
  blocking collectives  48.9 us (85%)
  matrix products  5.54 us (10%)
  other arithmetic  2.13 us (4%)
  local copies, waits for them, and re-layouts  0.61 us (1%)
    psum x1, blocking collectives, body(): summed = lax.psum(partial_value, 'gy')  16.7 us
    all_gather x1, blocking collectives, body(): full = lax.all_gather(agg, 'gz', axis=0, tiled=True)  14.2 us
    psum x1, blocking collectives, body(): lax.psum((jnp.sum(z_vals, axis=1), jnp.sum(z_vals * z_vals, axis=1)), ('g...  11.8 us
    all_gather x1, blocking collectives, body(): panel = lax.all_gather(features, 'gx', axis=1, tiled=True)  6.13 us
    dot_general x1, matrix products, body(): jnp.einsum('fcn,rcmn->frcm', panels, tiles, preferred_element_type=jnp.fl...  3.75 us
    dot_general x1, matrix products, body(): jnp.einsum('frcm,rc->frm', prods, share)  1.42 us

commit v1 on v0

--- a/solution.py
+++ b/solution.py
@@ -2,6 +2,22 @@
 import jax.numpy as jnp
 from jax import lax
 from jax.sharding import PartitionSpec as P
+
+
+def ring_product(value, axis, dim, term):
+    size, mine, span = (lax.axis_size(axis), lax.axis_index(axis), value.shape[dim])
+    forward = [(i, (i + 1) % size) for i in range(size)]
+    downward = [(i, (i - 1) % size) for i in range(size)]
+    half = size // 2
+    from_left = from_right = value
+    running = term(value, mine * span)
+    for hop in range(1, half + 1):
+        from_left = lax.ppermute(from_left, axis, forward)
+        if hop < size - half:
+            from_right = lax.ppermute(from_right, axis, downward)
+            running = running + term(from_right, (mine + hop) % size * span)
+        running = running + term(from_left, (mine - hop) % size * span)
+    return running
 
 
 def body(features, tiles, block_mask, tile_counts, weight, gamma, beta):
@@ -19,9 +35,18 @@
     agg = lax.dynamic_slice_in_dim(summed, lax.axis_index("gy") * width, width, 1)
     agg = agg.astype(jnp.bfloat16)
     offset = lax.axis_index("gz") * local_ch
-    full = lax.all_gather(agg, "gz", axis=0, tiled=True)
     w_cols = lax.dynamic_slice_in_dim(weight, offset, local_ch, 1)
-    z_vals = jnp.einsum("co,cn->on", w_cols, full, preferred_element_type=jnp.float32)
+    z_vals = ring_product(
+        agg,
+        "gz",
+        0,
+        lambda shard, start: jnp.einsum(
+            "co,cn->on",
+            lax.dynamic_slice_in_dim(w_cols, start, shard.shape[0], axis=0),
+            shard,
+            preferred_element_type=jnp.float32,
+        ),
+    )
     total = z_vals.shape[1] * lax.axis_size(("gx", "gy"))
     sums, squares = lax.psum(
         (jnp.sum(z_vals, axis=1), jnp.sum(z_vals * z_vals, axis=1)), ("gx", "gy")

time: 57.5 us -> 59.2 us (1.030)
  blocking collectives: 48.9 us -> 34.7 us
  waiting for transfers between devices: 0 us -> 11.2 us
  starting transfers between devices: 0 us -> 3.76 us
  matrix products: 5.54 us -> 6.34 us
    all_gather x1 -> x0, blocking collectives: 14.2 us -> none  [body(): full = lax.all_gather(agg, 'gz', axis=0, tiled=True)]
    ppermute x0 -> x3, waiting for transfers between devices: none -> 11.2 us  [the longest x2 11.2 us: ring_product(): from_left = lax.ppermute(from_left, axis, forward)]
    ppermute x0 -> x3, starting transfers between devices: none -> 3.76 us  [the longest x1 3.76 us: ring_product(): from_right = lax.ppermute(from_right, axis, downward)]
    dot_general x1 -> x4, matrix products: 0.37 us -> 1.17 us  [body(): jnp.einsum('co,cn->on', lax.dynamic_slice_in_dim(w_cols, start, shard.sha...]
  transfers between devices with their start and end apart: 0 -> 3, of which waited for: 0 -> 2; matrix products, arithmetic and copies ran while one was open for 0% -> 1% of each run, Pallas kernels for 0% -> 0%
where the time goes in v1:
time: 59.2 us; the launch traced here: 58.9 us
  blocking collectives  34.7 us (59%)
  waiting for transfers between devices  11.2 us (19%)
  matrix products  6.34 us (11%)
  starting transfers between devices  3.76 us (6%)
  other arithmetic  2.13 us (4%)
  local copies, waits for them, and re-layouts  0.61 us (1%)
    psum x1, blocking collectives, body(): summed = lax.psum(partial_value, 'gy')  16.7 us
    psum x1, blocking collectives, body(): lax.psum((jnp.sum(z_vals, axis=1), jnp.sum(z_vals * z_vals, axis=1)), ('g...  11.8 us
    ppermute x2, waiting for transfers between devices, ring_product(): from_left = lax.ppermute(from_left, axis, forward)  11.2 us
    all_gather x1, blocking collectives, body(): panel = lax.all_gather(features, 'gx', axis=1, tiled=True)  6.13 us
    ppermute x1, starting transfers between devices, ring_product(): from_right = lax.ppermute(from_right, axis, downward)  3.76 us
    dot_general x1, matrix products, body(): jnp.einsum('fcn,rcmn->frcm', panels, tiles, preferred_element_type=jnp.fl...  3.75 us
    dot_general x1, matrix products, body(): jnp.einsum('frcm,rc->frm', prods, share)  1.42 us
  transfers between devices with their start and end apart: 3, of which 2 were waited for; matrix products, arithmetic and copies ran while one was open for 1% of the time, Pallas kernels for 0%

profile of v1, /device:TPU:0, one launch (start us, length us, event | category | flops | bytes accessed | tf_op | source)
XLA Modules:
  0.0 58.9 jit_solution(16422485487506168689)
XLA Ops:
  0.0 0.0 copy-start
  0.0 0.7 %convert_element_type.13 = f32[16]{0:T(128)S(1)} convert(s32[16]{0:T(128)} %param.10) | non-fusion elementwise | flops 16 | bytes 128 | tf_op jit(solution)/shard_map/convert_element_type | solution.py:31
  0.7 0.7 %divide_bitcast_fusion = bf16[16,8,1,1]{0,1,2,3:T(8,128)(2,1)S(1)} fusion(s32[16,8]{0,1:T(8,128)} %param.9, f32[16]{0:T(128)S(1)} %convert_element_type.13), kind=kLoop, calls=%fused_computation.18 | loop fusion | flops 384 | bytes 832 | tf_op jit(solution)/shard_map/div | solution.py:31
  1.4 0.1 copy.12
  1.5 6.1 %all_gather.3 = bf16[64,1024]{1,0:T(8,128)(2,1)S(1)} all-gather(bf16[64,512]{1,0:T(8,128)(2,1)} %param.7), channel_id=1, replica_groups=mesh['gx'=2,'gy'=4,'gz'=4] {'gx'}, dimensions={1}, use_global_device_ids=true | all-gather | bytes 196608 | tf_op jit(solution)/shard_map/all_gather | solution.py:24
  7.6 3.8 %fusion.4 = bf16[64,16,8,128]{3,0,1,2:T(8,128)(2,1)S(1)} fusion(bf16[16,8,128,128]{3,2,1,0:T(8,128)(2,1)} %param.8, bf16[64,8,128,1]{2,1,0,3:T(8,128)(2,1)S(1)} %bitcast.22), kind=kOutput, calls=%fused_computation.4 | convolution fusion | flops 268435456 | bytes 6422528 | tf_op jit(solution)/shard_map/fcn,rcmn->frcm/dot_general | solution.py:30
  11.4 1.4 %fusion = f32[16,1,64,128]{3,1,2,0:T(1,128)S(1)} fusion(bf16[16,8,1,1]{1,2,3,0:T(2,128)(2,1)S(1)} %copy.12, bf16[64,16,8,128]{3,0,1,2:T(8,128)(2,1)S(1)} %fusion.4), kind=kOutput, calls=%fused_computation | convolution fusion | flops 2097152 | bytes 2621696 | tf_op jit(solution)/shard_map/frcm,rc->frm/dot_general | solution.py:32
  12.8 0.0 copy-start.1
  12.8 0.0 copy-start.2
  12.8 0.3 copy.14
  13.2 0.2 copy.28
  13.3 16.7 %all-reduce.2 = bf16[64,2048]{1,0:T(8,128)(2,1)S(1)} all-reduce(f32[64,2048]{1,0:T(8,128)S(1)} %bitcast.21), channel_id=1, replica_groups=mesh['gx'=2,'gy'=4,'gz'=4] {'gy'}, use_global_device_ids=true, to_apply=%region_0.0 | all-reduce | flops 131072 | bytes 786432 | tf_op jit(solution)/shard_map/psum | solution.py:33
  30.1 3.8 %collective-permute-start = (bf16[64,512]{1,0:T(8,128)(2,1)S(1)}, bf16[64,512]{1,0:T(8,128)(2,1)S(1)}, u32[]{:S(2)}, u32[]{:S(2)}) collective-permute-start(bf16[64,512]{1,0:T(8,128)(2,1)S(1)} %dynamic-slice_convert_fusion), channel_id=1, source_target_pairs={{0,3},{1,0},{2,1},{3,2},{4,7},{5,4},{6,5},{7,6},{8,11},{9,8},{10,9... | collective-permute-start | bytes 196616 | tf_op jit(solution)/shard_map/ppermute | solution.py:17
  33.9 0.0 collective-permute-start.1
  33.9 0.0 copy-done
  33.9 0.3 fusion.11
  34.2 5.7 %collective-permute-done.1 = bf16[64,512]{1,0:T(8,128)(2,1)S(1)} collective-permute-done((bf16[64,512]{1,0:T(8,128)(2,1)S(1)}, bf16[64,512]{1,0:T(8,128)(2,1)S(1)}, u32[]{:S(2)}, u32[]{:S(2)}) %collective-permute-start.1) | collective-permute-done | bytes 65568 | tf_op jit(solution)/shard_map/ppermute | solution.py:15
  39.9 0.0 collective-permute-start.2
  39.9 0.0 collective-permute-done
  39.9 0.3 convolution_add_fusion.2
  40.2 0.3 convolution_add_fusion.1
  40.5 5.5 %collective-permute-done.2 = bf16[64,512]{1,0:T(8,128)(2,1)S(1)} collective-permute-done((bf16[64,512]{1,0:T(8,128)(2,1)S(1)}, bf16[64,512]{1,0:T(8,128)(2,1)S(1)}, u32[]{:S(2)}, u32[]{:S(2)}) %collective-permute-start.2) | collective-permute-done | bytes 65568 | tf_op jit(solution)/shard_map/ppermute | solution.py:15
  46.0 0.4 fusion.13
  46.4 11.8 %all-reduce = (f32[64]{0:T(128)S(1)}, f32[64]{0:T(128)S(1)}) all-reduce(f32[64]{0:T(128)S(1)} %get-tuple-element.6, f32[64]{0:T(128)S(1)} %get-tuple-element.5), channel_id=1, replica_groups=mesh['gx'=2,'gy'=4,'gz'=4] {'gx','gy'}, use_global_device_ids=true, to_apply=%region_4.5 | all-reduce | flops 128 | bytes 1024 | tf_op jit(solution)/shard_map/psum | solution.py:51
  58.2 0.0 copy-done.1
  58.2 0.0 copy-done.2
  58.2 0.7 %maximum_convert_fusion = bf16[64,512]{1,0:T(8,128)(2,1)} fusion(f32[64,512]{1,0:T(8,128)S(1)} %get-tuple-element.11, f32[64]{0:T(128)S(1)} %copy-done.1, f32[64]{0:T(128)S(1)} %get-tuple-element.10, f32[64]{0:T(128)S(1)} %get-tuple-element.9, f32[64]{0:T(128)S(1)} %copy-done.2), kind=kLoop, calls=%fused_computation.10 | loop fusion | flops 196608 | bytes 197632 | tf_op jit(solution)/shard_map/convert_element_type | solution.py:58
  (3 shorter events, 0.0 us)
Async XLA Ops:
  0.0 33.9 %copy-start = (bf16[256,256]{1,0:T(8,128)(2,1)S(1)}, bf16[256,256]{1,0:T(8,128)(2,1)}, u32[]{:S(2)}) copy-start(bf16[256,256]{1,0:T(8,128)(2,1)} %param.11) | copy-start | bytes 393220
  12.8 45.4 %copy-start.1 = (f32[64]{0:T(128)S(1)}, f32[64]{0:T(128)}, u32[]{:S(2)}) copy-start(f32[64]{0:T(128)} %param.13) | copy-start | bytes 772
  12.8 45.4 %copy-start.2 = (f32[64]{0:T(128)S(1)}, f32[64]{0:T(128)}, u32[]{:S(2)}) copy-start(f32[64]{0:T(128)} %param.12) | copy-start | bytes 772
  30.1 9.8 %collective-permute-start = (bf16[64,512]{1,0:T(8,128)(2,1)S(1)}, bf16[64,512]{1,0:T(8,128)(2,1)S(1)}, u32[]{:S(2)}, u32[]{:S(2)}) collective-permute-start(bf16[64,512]{1,0:T(8,128)(2,1)S(1)} %dynamic-slice_convert_fusion), channel_id=1, source_target_pairs={{0,3},{1,0},{2,1},{3,2},{4,7},{5,4},{6,5},{7,6},{8,11},{9,8},{10,9... | collective-permute-start | bytes 196616 | tf_op jit(solution)/shard_map/ppermute | solution.py:17
  33.9 6.1 %collective-permute-start.1 = (bf16[64,512]{1,0:T(8,128)(2,1)S(1)}, bf16[64,512]{1,0:T(8,128)(2,1)S(1)}, u32[]{:S(2)}, u32[]{:S(2)}) collective-permute-start(bf16[64,512]{1,0:T(8,128)(2,1)S(1)} %dynamic-slice_convert_fusion), channel_id=1, source_target_pairs={{0,1},{1,2},{2,3},{3,0},{4,5},{5,6},{6,7},{7,4},{8,9},{9,10},{10,1... | collective-permute-start | bytes 196616 | tf_op jit(solution)/shard_map/ppermute | solution.py:15
  39.9 6.1 %collective-permute-start.2 = (bf16[64,512]{1,0:T(8,128)(2,1)S(1)}, bf16[64,512]{1,0:T(8,128)(2,1)S(1)}, u32[]{:S(2)}, u32[]{:S(2)}) collective-permute-start(bf16[64,512]{1,0:T(8,128)(2,1)S(1)} %collective-permute-done.1), channel_id=1, source_target_pairs={{0,1},{1,2},{2,3},{3,0},{4,5},{5,6},{6,7},{7,4},{8,9},{9,10},{10,1... | collective-permute-start | bytes 196616 | tf_op jit(solution)/shard_map/ppermute | solution.py:15
